TPU v7x, 32 devices: a whole 2x2x4 slice. The times are simulated.
32 devices in a mesh: groups: 2 (over y), seq: 4 (over z), beam: 4 (over x, core).
Axes of the slice: x: 2, y: 2, z: 4, core: 2. Of those that a mesh axis runs over, the one named last changes fastest.
Arguments:
- prompt_values: bfloat16 [2048, 8192], P(('groups', 'seq'), 'beam'), parts along dimension 0, may hold values from -6 to 6
- prompt_keys: bfloat16 [2048, 128], P(('groups', 'seq')), parts along dimension 0, may hold values from -0.31445312 to 0.31445312
- prompt_queries: bfloat16 [2048, 128], P(('groups', 'seq')), parts along dimension 0, may hold values from -0.31445312 to 0.31445312
- logarithm_state_decay: float32 [2048, 128], P(('groups', 'seq'), 'beam'), parts along dimension 0, may hold values from -1 to 0
- step_values: bfloat16 [8, 4, 8192], P('groups', 'beam', 'seq'), parts along dimension 0, may hold values from -6 to 6
- step_keys: bfloat16 [8, 4, 128], P('groups', 'beam'), parts along dimension 0, may hold values from -6 to 6
- step_queries: bfloat16 [8, 4, 128], P('groups', 'beam'), parts along dimension 0, may hold values from -0.31445312 to 0.31445312
- step_decay: float32 [8, 4, 128], P('groups', 'beam', 'seq'), parts along dimension 0, may hold values from -0.6 to -0.02
- step_logprob: float32 [8, 4], P('groups', 'beam'), parts along dimension 0, may hold values from -6 to -0.05
- parents: int32 [8, 4], P('groups', 'beam'), parts along dimension 0, may hold values from 0 to 3
- finished: int32 [8, 4], P('groups', 'beam'), parts along dimension 0, may hold values 0 or 1
- lengths: int32 [8], P(('groups', 'beam')), parts along dimension 0, may hold values from 1 to 59
- init_score: float32 [8], P(('groups', 'beam')), parts along dimension 0, may hold values from -20 to -2
Outputs:
- prompt_output: bfloat16 [2048, 8192], P(('groups', 'seq'), 'beam'), parts along dimension 0
- step_output: bfloat16 [8, 4, 8192], P('groups', 'beam', 'seq'), parts along dimension 0
- ranked: float32 [8, 4], P('groups', 'beam'), parts along dimension 0
- beam_states: float32 [8, 8192, 128], P(('groups', 'beam'), 'seq'), parts along dimension 0
There are 2 independent parts, one for each index of `groups`. A program takes and returns all parts, laid end to end along the dimension named above; each array names one. Nothing has to cross between parts.
All inputs are finite; a program needn't handle non-finite values. No bound on the sum of `finished` on one device may be relied on, other than what follows from the above.
Results may differ from a plain program's by a relative error of at most 0.0056.
Values sent between devices are 32-bit elements; how exact they have to be, the bound alone decides.
No kernel may reach another device: no remote copies, remote signals or barrier semaphores. Data moves between devices by JAX's collectives and lax.ppermute only.
A program may use at most 64 MiB of HBM per device.

v0:
```python
import jax
import jax.numpy as jnp
from jax import lax
from jax.sharding import PartitionSpec as P

P_SIZE = 64
N = 128
STEPS = 4
SPAN = 256


def on_device(
    prompt_values,
    prompt_keys,
    prompt_queries,
    logarithm_state_decay,
    step_values,
    step_keys,
    step_queries,
    step_decay,
    step_logprob,
    parents,
    finished,
    lengths,
    init_score,
):
    token_rows = prompt_values.shape[0]
    head_count = logarithm_state_decay.shape[1]
    block_count = token_rows // SPAN
    values_blocks = prompt_values.reshape(block_count, SPAN, head_count, P_SIZE)
    keys_blocks = prompt_keys.reshape(block_count, SPAN, N)
    query_blocks = prompt_queries.reshape(block_count, SPAN, N)
    decay_sums = jnp.cumsum(logarithm_state_decay.reshape(block_count, SPAN, head_count), axis=1)
    lower = jnp.tril(jnp.ones((SPAN, SPAN), dtype=bool))

    def within(item):
        values_one, keys_one, query_one, sums_one = item
        scores = jnp.dot(query_one, keys_one.T, preferred_element_type=jnp.float32)
        spread = jnp.where(lower[:, :, None], sums_one[:, None, :] - sums_one[None, :, :], -jnp.inf)
        weights = (scores[:, :, None] * jnp.exp(spread)).astype(jnp.bfloat16)
        return jnp.einsum("ijh,jhp->ihp", weights, values_one, preferred_element_type=jnp.float32)

    inner_out = lax.map(within, (values_blocks, keys_blocks, query_blocks, decay_sums))
    tail_decay = jnp.exp(decay_sums[:, -1:, :] - decay_sums)
    scaled = (values_blocks * tail_decay[:, :, :, None]).astype(jnp.bfloat16)
    block_states = jnp.einsum(
        "kjhp,kjn->khpn", scaled, keys_blocks, preferred_element_type=jnp.float32
    )
    block_decay = jnp.exp(decay_sums[:, -1, :])

    def advance(carry, item):
        state_now, current_shrink_factor = carry
        single_token_decay, state_one = item
        return (
            (
                single_token_decay[:, None, None] * state_now + state_one,
                current_shrink_factor * single_token_decay,
            ),
            (state_now, current_shrink_factor),
        )

    zero_state = jnp.zeros((head_count, P_SIZE, N), jnp.float32)
    unit_decay = jnp.ones((head_count,), jnp.float32)
    (segment_finish, total_decay), (before, prior) = lax.scan(
        advance, (zero_state, unit_decay), (block_decay, block_states)
    )
    seq_index = lax.axis_index("seq")
    all_decays, all_states = (
        lax.all_gather(total_decay[None], "seq", axis=0, tiled=True),
        lax.all_gather(segment_finish[None], "seq", axis=0, tiled=True),
    )
    piece_ids = jnp.arange(all_decays.shape[0], dtype=jnp.int32)

    def collect(carry, item):
        running, mine = carry
        decay_one, state_one, piece_id = item
        mine = jnp.where(piece_id == seq_index, running, mine)
        running = decay_one[:, None, None] * running + state_one
        return ((running, mine), None)

    (full_block, arriving_input), unused = lax.scan(
        collect, (zero_state, zero_state), (all_decays, all_states, piece_ids)
    )
    starts = prior[:, :, None, None] * arriving_input[None] + before
    carried = (
        jnp.einsum(
            "kin,khpn->kihp",
            query_blocks,
            starts.astype(jnp.bfloat16),
            preferred_element_type=jnp.float32,
        )
        * jnp.exp(decay_sums)[:, :, :, None]
    )
    prompt_output = (
        (inner_out + carried).astype(jnp.bfloat16).reshape(token_rows, head_count * P_SIZE)
    )
    group_heads = step_values.shape[2] // P_SIZE
    first_head = seq_index * group_heads
    every_head = lax.all_gather(full_block, "beam", axis=0, tiled=True)
    own_heads = lax.dynamic_slice_in_dim(every_head, first_head, group_heads, 0)
    state_now = own_heads
    score_now = init_score
    length_now = lengths.astype(jnp.float32)
    step_list = []
    ranked_list = []
    for step_index in range(STEPS):
        parent_now = parents[step_index, 0]
        pieces = (
            lax.all_gather(state_now[None], "beam", axis=0, tiled=True),
            lax.all_gather(score_now, "beam", axis=0, tiled=True),
            lax.all_gather(length_now, "beam", axis=0, tiled=True),
        )
        slot_ids = jnp.arange(pieces[0].shape[0], dtype=jnp.int32)
        picked = (slot_ids == parent_now).astype(jnp.float32)
        state_part = jnp.sum(picked[:, None, None, None] * pieces[0], axis=0, keepdims=True)
        score_part = jnp.sum(picked * pieces[1]).reshape(1)
        length_part = jnp.sum(picked * pieces[2]).reshape(1)
        done = finished[step_index, 0] == 1
        live = (1 - finished[step_index]).astype(jnp.float32)
        values_now = step_values[step_index, 0].astype(jnp.float32).reshape(group_heads, P_SIZE)
        keys_now = step_keys[step_index, 0].astype(jnp.float32)
        updated = (
            jnp.exp(step_decay[step_index, 0])[:, None, None] * state_part[0]
            + values_now[:, :, None] * keys_now[None, None, :]
        )
        state_now = jnp.where(done, state_part[0], updated)
        output_now = jnp.einsum(
            "hpn,n->hp",
            state_now.astype(jnp.bfloat16),
            step_queries[step_index, 0],
            preferred_element_type=jnp.float32,
        )
        output_now = jnp.where(done, jnp.float32(0.0), output_now)
        step_list.append(output_now.reshape(1, group_heads * P_SIZE).astype(jnp.bfloat16))
        score_now = score_part + live * step_logprob[step_index]
        length_now = length_part + live
        normed = score_now / ((5.0 + length_now) / 6.0) ** 0.6
        best = lax.pmax(normed, "beam")
        ranked_list.append(normed - best)
    step_output = jnp.stack(step_list)
    ranked = jnp.stack(ranked_list)
    beam_states = state_now.reshape(1, group_heads * P_SIZE, N)
    return (prompt_output, step_output, ranked, beam_states)


def solution(mesh):
    return jax.shard_map(
        on_device,
        mesh=mesh,
        in_specs=(
            P(("groups", "seq"), "beam"),
            P(("groups", "seq"), None),
            P(("groups", "seq"), None),
            P(("groups", "seq"), "beam"),
            P("groups", "beam", "seq"),
            P("groups", "beam", None),
            P("groups", "beam", None),
            P("groups", "beam", "seq"),
            P("groups", "beam"),
            P("groups", "beam"),
            P("groups", "beam"),
            P(("groups", "beam")),
            P(("groups", "beam")),
        ),
        out_specs=(
            P(("groups", "seq"), "beam"),
            P("groups", "beam", "seq"),
            P("groups", "beam"),
            P(("groups", "beam"), "seq", None),
        ),
        check_vma=False,
    )
```

profile of v0, /device:TPU:0, one launch (start us, length us, event | category | flops | bytes accessed | tf_op | source)
XLA Modules:
  0.0 360.7 jit_solution(6325629616704435772)
XLA Ops:
  9.1 1.5 copy.50
  12.3 12.6 %all-gather = f32[4,1,32]{2,1,0:T(1,128)S(1)} all-gather(f32[1,1,32]{2,1,0:T(1,128)S(1)} %get-tuple-element.163), channel_id=2, replica_groups=mesh['groups'=2,'seq'=4,'beam'=4] {'seq'}, dimensions={0}, use_global_device_ids=true | all-gather | bytes 640 | tf_op jit(solution)/shard_map/all_gather | solution.py:69
  25.0 70.9 %all-gather.18.cloned.1.call-done = f32[128,64,128]{2,1,0:T(8,128)} async-done(((f32[32,64,128]{2,1,0:T(8,128)}), f32[128,64,128]{2,1,0:T(8,128)}) %all-gather.18.cloned.1.call-update) | async-done | bytes 4194320 | tf_op jit(solution)/shard_map/all_gather | solution.py:70
  95.9 11.8 %while.3 = (s32[]{:T(128)}, f32[32,64,128]{2,1,0:T(8,128)S(1)}, bf16[32,64,128]{2,1,0:T(8,128)(2,1)S(1)}, f32[4,32]{1,0:T(4,128)S(1)}, f32[4,32,64,128]{3,2,1,0:...) while((s32[]{:T(128)}, f32[32,64,128]{2,1,0:T(8,128)S(1)}, ...), condition=%wide.region_3.4_spmd.clone, body=%wide.region_2.3_spmd.clone.sunk | while | flops 1572868 | bytes 5243406 | solution.py:81
  97.4 1.4 bitcast_add_fusion.7
  100.3 1.4 bitcast_add_fusion.7
  103.3 1.4 bitcast_add_fusion.7
  106.2 1.4 bitcast_add_fusion.7
  108.7 33.0 %all-gather.10.cloned.1.call-done = f32[128,64,128]{2,1,0:T(8,128)} async-done(((f32[32,64,128]{2,1,0:T(8,128)}), f32[128,64,128]{2,1,0:T(8,128)}) %all-gather.10.cloned.1.call-update) | async-done | bytes 4194320 | tf_op jit(solution)/shard_map/all_gather | solution.py:99
  141.8 2.3 constant_dynamic-slice_fusion
  146.9 31.8 %all-gather.20.cloned.1.call-done = f32[128,64,128]{2,1,0:T(8,128)} async-done(((f32[32,64,128]{2,1,0:T(8,128)}), f32[128,64,128]{2,1,0:T(8,128)}) %all-gather.20.cloned.1.call-update) | async-done | bytes 4194320 | tf_op jit(solution)/shard_map/all_gather | solution.py:109
  178.7 2.9 multiply_reduce_fusion.3
  184.4 33.2 %all-gather.12.cloned.1.call-done = f32[4,32,64,128]{3,2,1,0:T(8,128)} async-done(((f32[1,32,64,128]{3,2,1,0:T(8,128)}), f32[4,32,64,128]{3,2,1,0:T(8,128)}) %all-gather.12.cloned.1.call-update) | async-done | bytes 4194320 | tf_op jit(solution)/shard_map/all_gather | solution.py:109
  217.6 2.9 multiply_reduce_fusion.2
  224.2 33.2 %all-gather.14.cloned.1.call-done = f32[4,32,64,128]{3,2,1,0:T(8,128)} async-done(((f32[1,32,64,128]{3,2,1,0:T(8,128)}), f32[4,32,64,128]{3,2,1,0:T(8,128)}) %all-gather.14.cloned.1.call-update) | async-done | bytes 4194320 | tf_op jit(solution)/shard_map/all_gather | solution.py:109
  257.4 2.9 multiply_reduce_fusion.1
  266.1 5.9 %all-reduce.11 = (f32[4]{0:T(128)S(1)}, f32[4]{0:T(128)S(1)}) all-reduce(f32[4]{0:T(128)S(1)} %dynamic-update-slice, f32[4]{0:T(128)S(1)} %convert_dynamic-update-slice_fusion), channel_id=1, replica_groups=mesh['groups'=2,'seq'=4,'beam'=4] {'beam'}, use_global_device_ids=true, to_apply=%add | all-reduce | flops 8 | bytes 64
  276.5 1.7 fusion.50
  278.2 1.4 dynamic-update-slice.2
  279.7 1.4 dynamic-update-slice.3
  281.1 6.5 %all-reduce.10 = (f32[4]{0:T(128)S(1)}, f32[4]{0:T(128)S(1)}) all-reduce(f32[4]{0:T(128)S(1)} %dynamic-update-slice.2, f32[4]{0:T(128)S(1)} %dynamic-update-slice.3), channel_id=1, replica_groups=mesh['groups'=2,'seq'=4,'beam'=4] {'beam'}, use_global_device_ids=true, to_apply=%add.2 | all-reduce | flops 8 | bytes 64
  292.6 1.7 fusion.48
  295.7 1.4 dynamic-update-slice.5
  297.1 6.1 %all-reduce.9 = (f32[4]{0:T(128)S(1)}, f32[4]{0:T(128)S(1)}) all-reduce(f32[4]{0:T(128)S(1)} %dynamic-update-slice.4, f32[4]{0:T(128)S(1)} %dynamic-update-slice.5), channel_id=1, replica_groups=mesh['groups'=2,'seq'=4,'beam'=4] {'beam'}, use_global_device_ids=true, to_apply=%add.4 | all-reduce | flops 8 | bytes 64
  308.2 1.9 fusion.46
  312.8 6.1 %all-reduce.8 = (f32[4]{0:T(128)S(1)}, f32[4]{0:T(128)S(1)}) all-reduce(f32[4]{0:T(128)S(1)} %dynamic-update-slice.6, f32[4]{0:T(128)S(1)} %dynamic-update-slice.7), channel_id=1, replica_groups=mesh['groups'=2,'seq'=4,'beam'=4] {'beam'}, use_global_device_ids=true, to_apply=%add.6 | all-reduce | flops 8 | bytes 64
  324.2 7.0 %all-reduce.12 = (f32[1]{0:T(128)}, f32[1]{0:T(128)}, f32[1]{0:T(128)}, f32[1]{0:T(128)}) all-reduce(f32[1]{0:T(128)S(6)} %div.31, f32[1]{0:T(128)} %get-tuple-element.186, f32[1]{0:T(128)} %get-tuple-element.190, f32[1]{0:T(128)} %get-tuple-element.194), channel_id=1, replica_groups=mesh['groups'=2,'seq'=4,'beam'=4] {'beam'}, use_global_device_ids=true, to_apply=%region_19.20 | all-reduce | flops 4 | bytes 32 | tf_op jit(solution)/shard_map/pmax | solution.py:138
  338.7 3.7 %fusion.7 = bf16[256,32,64]{0,2,1:T(8,128)(2,1)} fusion(f32[32,64,256]{2,1,0:T(8,128)S(1)} %fusion.13, bf16[256,32,64]{0,2,1:T(8,128)(2,1)S(1)} %bitcast.193, f32[256,32]{0,1:T(8,128)S(1)} %copy.48, f32[256,256]{1,0:T(8,128)S(1)} %fusion.51, pred[256,256]{1,0:T(8,128)(4,1)S(1)} %iota_compare_fusion, f32[256,32]{0,1:T(8,128)S(1)} %copy.53), kind=kOutput, calls=%fused_computation.16 | convolution fusion | flops 278396928 | bytes 4587520 | tf_op jit(solution)/shard_map/while/body/eval_jaxpr/ijh,jhp->ihp/dot_general | solution.py:41
  342.4 2.4 copy.54
  345.4 1.8 fusion.16
  348.0 2.9 multiply_reduce_fusion
  351.6 1.6 bitcast_select_fusion
  (132 shorter events, 42.0 us)
Async XLA Ops:
  7.2 330.8 %copy-start = (bf16[256,128]{1,0:T(8,128)(2,1)S(1)}, bf16[256,128]{1,0:T(8,128)(2,1)}, u32[]{:S(2)}) copy-start(bf16[256,128]{1,0:T(8,128)(2,1)} %param.17) | copy-start | bytes 196612
  7.2 3.6 %copy-start.5 = (bf16[256,128]{1,0:T(8,128)(2,1)S(1)}, bf16[256,128]{1,0:T(8,128)(2,1)}, u32[]{:S(2)}) copy-start(bf16[256,128]{1,0:T(8,128)(2,1)} %param.16) | copy-start | bytes 196612
  7.2 88.7 %all-gather.18.cloned.1.call-start = ((), (), s32[]{:S(2)}) async-start(), calls=%async_computation.4 | async-start | bytes 5242880 | tf_op jit(solution)/shard_map/all_gather | solution.py:70
  12.3 129.5 %all-gather.10.cloned.1.call-start = ((), (), s32[]{:S(2)}) async-start(), calls=%async_computation | async-start | bytes 5242880 | tf_op jit(solution)/shard_map/all_gather | solution.py:99
  107.7 1.0 copy-start.1
  107.7 36.5 %copy-start.6 = (bf16[4,1,2048]{2,0,1:T(4,128)(2,1)S(1)}, bf16[4,1,2048]{2,0,1:T(4,128)(2,1)}, u32[]{:S(2)}) copy-start(bf16[4,1,2048]{2,0,1:T(4,128)(2,1)} %param.19) | copy-start | bytes 49156
  107.7 36.6 %copy-start.7 = (s32[4,1]{0,1:T(1,128)S(1)}, s32[4,1]{0,1:T(1,128)}, u32[]{:S(2)}) copy-start(s32[4,1]{0,1:T(1,128)} %param.25) | copy-start | bytes 52
  107.7 37.9 %copy-start.8 = (s32[4,1]{0,1:T(1,128)S(1)}, s32[4,1]{0,1:T(1,128)}, u32[]{:S(2)}) copy-start(s32[4,1]{0,1:T(1,128)} %param.24) | copy-start | bytes 52
  107.7 39.2 %copy-start.11 = (f32[4,1,32]{2,1,0:T(1,128)S(1)}, f32[4,1,32]{2,1,0:T(1,128)}, u32[]{:S(2)}) copy-start(f32[4,1,32]{2,1,0:T(1,128)} %param.22) | copy-start | bytes 1540
  107.7 39.2 %copy-start.10 = (bf16[4,1,128]{2,0,1:T(4,128)(2,1)S(1)}, bf16[4,1,128]{2,0,1:T(4,128)(2,1)}, u32[]{:S(2)}) copy-start(bf16[4,1,128]{2,0,1:T(4,128)(2,1)} %param.20) | copy-start | bytes 3076
  108.7 70.0 %all-gather.20.cloned.1.call-start = ((), (), s32[]{:S(2)}) async-start(), calls=%async_computation.5 | async-start | bytes 5242880 | tf_op jit(solution)/shard_map/all_gather | solution.py:109
  144.1 73.5 %all-gather.12.cloned.1.call-start = ((), (), s32[]{:S(2)}) async-start(), calls=%async_computation.1 | async-start | bytes 5242880 | tf_op jit(solution)/shard_map/all_gather | solution.py:109
  183.0 74.5 %all-gather.14.cloned.1.call-start = ((), (), s32[]{:S(2)}) async-start(), calls=%async_computation.2 | async-start | bytes 5242880 | tf_op jit(solution)/shard_map/all_gather | solution.py:109
  220.5 1.0 copy-start.2
  222.8 125.2 %all-gather.16.cloned.1.call-start = ((), (), s32[]{:S(2)}) async-start(), calls=%async_computation.3 | async-start | bytes 5242880 | tf_op jit(solution)/shard_map/all_gather | solution.py:109
  224.2 39.8 %copy-start.13 = (u32[32]{0:T(128)S(1)}, u32[32]{0:T(128)}, u32[]{:S(2)}) copy-start(u32[32]{0:T(128)} %constant.105) | copy-start | bytes 388
  224.2 51.6 %copy-start.9 = (f32[4,1]{0,1:T(1,128)S(1)}, f32[4,1]{0,1:T(1,128)}, u32[]{:S(2)}) copy-start(f32[4,1]{0,1:T(1,128)} %param.23) | copy-start | bytes 52
  260.3 1.0 copy-start.3
  338.7 6.1 %copy-start.12 = (bf16[4,1,128]{2,0,1:T(4,128)(2,1)S(1)}, bf16[4,1,128]{2,0,1:T(4,128)(2,1)}, u32[]{:S(2)}) copy-start(bf16[4,1,128]{2,0,1:T(4,128)(2,1)} %param.21) | copy-start | bytes 3076
  342.4 5.0 %copy-start.4 = (f32[32,64,128]{2,1,0:T(8,128)S(1)}, f32[32,64,128]{2,1,0:T(8,128)}, u32[]{:S(2)}) copy-start(f32[32,64,128]{2,1,0:T(8,128)} %copy-done.3) | copy-start | bytes 3145732
Sparse Core Ops, SparseCore 0:
  12.4 83.4 all-gather.17
  108.8 32.9 all-gather.9
  144.2 34.4 all-gather.19
  183.1 34.4 all-gather.11
  222.9 34.4 all-gather.13
  262.9 34.5 all-gather.15
where the time goes:
time: 362 us; the launch traced here: 361 us
  waiting for transfers between devices  202 us (56%)
  other arithmetic  47.2 us (13%)
  blocking collectives  44.2 us (12%)
  between operations  29.5 us (8%)
  local copies, waits for them, and re-layouts  25.3 us (7%)
  matrix products  9.29 us (3%)
    all_gather x4, waiting for transfers between devices, on_device(): lax.all_gather(state_now[None], 'beam', axis=0, tiled=True)  98.2 us
    all_gather x1, waiting for transfers between devices, on_device(): lax.all_gather(segment_finish[None], 'seq', axis=0, tiled=True)  70.9 us
    all_gather x1, waiting for transfers between devices, on_device(): every_head = lax.all_gather(full_block, 'beam', axis=0, tiled=True)  33 us
    unnamed x4, blocking collectives  24.6 us
    unnamed x46, local copies, waits for them, and re-layouts  16.5 us
    all_gather x1, blocking collectives, on_device(): lax.all_gather(total_decay[None], 'seq', axis=0, tiled=True)  12.6 us
    reduce_sum x4, other arithmetic, on_device(): jnp.sum(picked[:, None, None, None] * pieces[0], axis=0, keepdims=True)  11.5 us
  transfers between devices with their start and end apart: 6, of which 5 were waited for; matrix products, arithmetic and copies ran while one was open for 12% of the time, Pallas kernels for 0%

commit v1 on v0

--- a/solution.py
+++ b/solution.py
@@ -96,7 +96,12 @@
     )
     group_heads = step_values.shape[2] // P_SIZE
     first_head = seq_index * group_heads
-    every_head = lax.all_gather(full_block, "beam", axis=0, tiled=True)
+    ring = [full_block]
+    for hop in range(3):
+        ring.append(lax.ppermute(ring[-1], "beam", [(dev, (dev + 1) % 4) for dev in range(4)]))
+    every_head = jnp.roll(
+        jnp.concatenate(ring[::-1], axis=0), (lax.axis_index("beam") + 1) * ring[0].shape[0], axis=0
+    )
     own_heads = lax.dynamic_slice_in_dim(every_head, first_head, group_heads, 0)
     state_now = own_heads
     score_now = init_score

time: 362 us -> 378 us (1.044)
  waiting for transfers between devices: 202 us -> 211 us
  local copies, waits for them, and re-layouts: 25.3 us -> 31 us
    ppermute x0 -> x3, waiting for transfers between devices: none -> 43.1 us  [on_device(): lax.ppermute(ring[-1], 'beam', [(dev, (dev + 1) % 4) for dev in range(4)])]
    all_gather x1 -> x0, waiting for transfers between devices: 33 us -> none  [on_device(): every_head = lax.all_gather(full_block, 'beam', axis=0, tiled=True)]
    unnamed x46 -> x53, local copies, waits for them, and re-layouts: 16.5 us -> 23.4 us
  transfers between devices with their start and end apart: 6 -> 8, of which waited for: 5 -> 7; matrix products, arithmetic and copies ran while one was open for 12% -> 12% of each run, Pallas kernels for 0% -> 0%
where the time goes in v1:
time: 378 us; the launch traced here: 377 us
  waiting for transfers between devices  211 us (56%)
  other arithmetic  47.2 us (12%)
  blocking collectives  44.2 us (12%)
  local copies, waits for them, and re-layouts  31 us (8%)
  between operations  29.3 us (8%)
  matrix products  11.4 us (3%)
    all_gather x4, waiting for transfers between devices, on_device(): lax.all_gather(state_now[None], 'beam', axis=0, tiled=True)  96.6 us
    all_gather x1, waiting for transfers between devices, on_device(): lax.all_gather(segment_finish[None], 'seq', axis=0, tiled=True)  70.9 us
    ppermute x3, waiting for transfers between devices, on_device(): lax.ppermute(ring[-1], 'beam', [(dev, (dev + 1) % 4) for dev in range(4)])  43.1 us
    unnamed x4, blocking collectives  24.6 us
    unnamed x53, local copies, waits for them, and re-layouts  23.4 us
    all_gather x1, blocking collectives, on_device(): lax.all_gather(total_decay[None], 'seq', axis=0, tiled=True)  12.6 us
    reduce_sum x4, other arithmetic, on_device(): jnp.sum(picked[:, None, None, None] * pieces[0], axis=0, keepdims=True)  11.5 us
  transfers between devices with their start and end apart: 8, of which 7 were waited for; matrix products, arithmetic and copies ran while one was open for 12% of the time, Pallas kernels for 0%

profile of v1, /device:TPU:0, one launch (start us, length us, event | category | flops | bytes accessed | tf_op | source)
XLA Modules:
  0.0 376.8 jit_solution(14266334318178534968)
XLA Ops:
  9.0 1.5 copy.50
  10.8 2.2 convolution_add_fusion
  13.1 12.6 %all-gather = f32[4,1,32]{2,1,0:T(1,128)S(1)} all-gather(f32[1,1,32]{2,1,0:T(1,128)S(1)} %get-tuple-element.163), channel_id=2, replica_groups=mesh['groups'=2,'seq'=4,'beam'=4] {'seq'}, dimensions={0}, use_global_device_ids=true | all-gather | bytes 640 | tf_op jit(solution)/shard_map/all_gather | solution.py:69
  25.8 70.9 %all-gather.15.cloned.1.call-done = f32[128,64,128]{2,1,0:T(8,128)} async-done(((f32[32,64,128]{2,1,0:T(8,128)}), f32[128,64,128]{2,1,0:T(8,128)}) %all-gather.15.cloned.1.call-update) | async-done | bytes 4194320 | tf_op jit(solution)/shard_map/all_gather | solution.py:70
  96.7 11.8 %while.3 = (s32[]{:T(128)}, f32[32,64,128]{2,1,0:T(8,128)S(1)}, bf16[32,64,128]{2,1,0:T(8,128)(2,1)S(1)}, f32[4,32]{1,0:T(4,128)S(1)}, f32[4,32,64,128]{3,2,1,0:...) while((s32[]{:T(128)}, f32[32,64,128]{2,1,0:T(8,128)S(1)}, ...), condition=%wide.region_3.4_spmd.clone, body=%wide.region_2.3_spmd.clone.sunk | while | flops 1572868 | bytes 5243406 | solution.py:81
  98.2 1.4 bitcast_add_fusion.7
  108.5 14.2 %collective-permute-done = f32[32,64,128]{2,1,0:T(8,128)S(1)} collective-permute-done((f32[32,64,128]{2,1,0:T(8,128)S(1)}, f32[32,64,128]{2,1,0:T(8,128)S(1)}, u32[]{:S(2)}, u32[]{:S(2)}) %collective-permute-start) | collective-permute-done | bytes 1048608 | tf_op jit(solution)/shard_map/ppermute | solution.py:101
  123.7 14.3 %collective-permute-done.1 = f32[32,64,128]{2,1,0:T(8,128)} collective-permute-done((f32[32,64,128]{2,1,0:T(8,128)S(1)}, f32[32,64,128]{2,1,0:T(8,128)}, u32[]{:S(2)}, u32[]{:S(2)}) %collective-permute-start.1) | collective-permute-done | bytes 1048608 | tf_op jit(solution)/shard_map/ppermute | solution.py:101
  138.0 14.5 %collective-permute-done.2 = f32[32,64,128]{2,1,0:T(8,128)} collective-permute-done((f32[32,64,128]{2,1,0:T(8,128)}, f32[32,64,128]{2,1,0:T(8,128)}, u32[]{:S(2)}, u32[]{:S(2)}) %collective-permute-start.2) | collective-permute-done | bytes 1048608 | tf_op jit(solution)/shard_map/ppermute | solution.py:101
  163.6 30.2 %all-gather.17.cloned.1.call-done = f32[128,64,128]{2,1,0:T(8,128)} async-done(((f32[32,64,128]{2,1,0:T(8,128)}), f32[128,64,128]{2,1,0:T(8,128)}) %all-gather.17.cloned.1.call-update) | async-done | bytes 4194320 | tf_op jit(solution)/shard_map/all_gather | solution.py:114
  193.8 2.9 multiply_reduce_fusion.3
  199.5 33.2 %all-gather.9.cloned.1.call-done = f32[4,32,64,128]{3,2,1,0:T(8,128)} async-done(((f32[1,32,64,128]{3,2,1,0:T(8,128)}), f32[4,32,64,128]{3,2,1,0:T(8,128)}) %all-gather.9.cloned.1.call-update) | async-done | bytes 4194320 | tf_op jit(solution)/shard_map/all_gather | solution.py:114
  232.7 2.9 multiply_reduce_fusion.2
  239.3 33.2 %all-gather.11.cloned.1.call-done = f32[4,32,64,128]{3,2,1,0:T(8,128)} async-done(((f32[1,32,64,128]{3,2,1,0:T(8,128)}), f32[4,32,64,128]{3,2,1,0:T(8,128)}) %all-gather.11.cloned.1.call-update) | async-done | bytes 4194320 | tf_op jit(solution)/shard_map/all_gather | solution.py:114
  272.5 2.9 multiply_reduce_fusion.1
  281.3 5.9 %all-reduce.11 = (f32[4]{0:T(128)S(1)}, f32[4]{0:T(128)S(1)}) all-reduce(f32[4]{0:T(128)S(1)} %dynamic-update-slice, f32[4]{0:T(128)S(1)} %convert_dynamic-update-slice_fusion), channel_id=1, replica_groups=mesh['groups'=2,'seq'=4,'beam'=4] {'beam'}, use_global_device_ids=true, to_apply=%add | all-reduce | flops 8 | bytes 64
  291.6 1.7 fusion.50
  293.4 1.4 dynamic-update-slice.2
  294.8 1.4 dynamic-update-slice.3
  296.2 6.5 %all-reduce.10 = (f32[4]{0:T(128)S(1)}, f32[4]{0:T(128)S(1)}) all-reduce(f32[4]{0:T(128)S(1)} %dynamic-update-slice.2, f32[4]{0:T(128)S(1)} %dynamic-update-slice.3), channel_id=1, replica_groups=mesh['groups'=2,'seq'=4,'beam'=4] {'beam'}, use_global_device_ids=true, to_apply=%add.2 | all-reduce | flops 8 | bytes 64
  307.7 1.7 fusion.48
  310.8 1.4 dynamic-update-slice.5
  312.3 6.1 %all-reduce.9 = (f32[4]{0:T(128)S(1)}, f32[4]{0:T(128)S(1)}) all-reduce(f32[4]{0:T(128)S(1)} %dynamic-update-slice.4, f32[4]{0:T(128)S(1)} %dynamic-update-slice.5), channel_id=1, replica_groups=mesh['groups'=2,'seq'=4,'beam'=4] {'beam'}, use_global_device_ids=true, to_apply=%add.4 | all-reduce | flops 8 | bytes 64
  323.4 1.9 fusion.46
  328.1 6.1 %all-reduce.8 = (f32[4]{0:T(128)S(1)}, f32[4]{0:T(128)S(1)}) all-reduce(f32[4]{0:T(128)S(1)} %dynamic-update-slice.6, f32[4]{0:T(128)S(1)} %dynamic-update-slice.7), channel_id=1, replica_groups=mesh['groups'=2,'seq'=4,'beam'=4] {'beam'}, use_global_device_ids=true, to_apply=%add.6 | all-reduce | flops 8 | bytes 64
  339.4 7.0 %all-reduce.12 = (f32[1]{0:T(128)}, f32[1]{0:T(128)}, f32[1]{0:T(128)}, f32[1]{0:T(128)}) all-reduce(f32[1]{0:T(128)S(6)} %div.31, f32[1]{0:T(128)} %get-tuple-element.186, f32[1]{0:T(128)} %get-tuple-element.190, f32[1]{0:T(128)} %get-tuple-element.194), channel_id=1, replica_groups=mesh['groups'=2,'seq'=4,'beam'=4] {'beam'}, use_global_device_ids=true, to_apply=%region_19.20 | all-reduce | flops 4 | bytes 32 | tf_op jit(solution)/shard_map/pmax | solution.py:143
  353.9 3.7 fusion.7
  357.6 2.3 copy.54
  360.6 1.8 fusion.16
  362.5 1.8 fusion.17
  364.4 2.9 multiply_reduce_fusion
  368.0 1.6 bitcast_select_fusion
  (143 shorter events, 52.5 us)
Async XLA Ops:
  7.2 346.1 %copy-start = (bf16[256,128]{1,0:T(8,128)(2,1)S(1)}, bf16[256,128]{1,0:T(8,128)(2,1)}, u32[]{:S(2)}) copy-start(bf16[256,128]{1,0:T(8,128)(2,1)} %param.17) | copy-start | bytes 196612
  7.2 89.5 %all-gather.15.cloned.1.call-start = ((), (), s32[]{:S(2)}) async-start(), calls=%async_computation.3 | async-start | bytes 5242880 | tf_op jit(solution)/shard_map/all_gather | solution.py:70
  13.0 180.8 %all-gather.17.cloned.1.call-start = ((), (), s32[]{:S(2)}) async-start(), calls=%async_computation.4 | async-start | bytes 5242880 | tf_op jit(solution)/shard_map/all_gather | solution.py:114
  108.5 14.3 %collective-permute-start = (f32[32,64,128]{2,1,0:T(8,128)S(1)}, f32[32,64,128]{2,1,0:T(8,128)S(1)}, u32[]{:S(2)}, u32[]{:S(2)}) collective-permute-start(f32[32,64,128]{2,1,0:T(8,128)S(1)} %get-tuple-element.85), channel_id=1, source_target_pairs={{0,1},{1,2},{2,3},{3,0},{4,5},{5,6},{6,7},{7,4},{8,9},{9,10},{10,1... | collective-permute-start | bytes 3145736 | tf_op jit(solution)/shard_map/ppermute | solution.py:101
  122.7 1.0 copy-start.1
  123.7 14.3 %collective-permute-start.1 = (f32[32,64,128]{2,1,0:T(8,128)S(1)}, f32[32,64,128]{2,1,0:T(8,128)}, u32[]{:S(2)}, u32[]{:S(2)}) collective-permute-start(f32[32,64,128]{2,1,0:T(8,128)S(1)} %collective-permute-done), channel_id=1, source_target_pairs={{0,1},{1,2},{2,3},{3,0},{4,5},{5,6},{6,7},{7,4},{8,9},{9,10},{10,1... | collective-permute-start | bytes 3145736 | tf_op jit(solution)/shard_map/ppermute | solution.py:101
  138.0 14.5 %collective-permute-start.2 = (f32[32,64,128]{2,1,0:T(8,128)}, f32[32,64,128]{2,1,0:T(8,128)}, u32[]{:S(2)}, u32[]{:S(2)}) collective-permute-start(f32[32,64,128]{2,1,0:T(8,128)} %collective-permute-done.1), channel_id=1, source_target_pairs={{0,1},{1,2},{2,3},{3,0},{4,5},{5,6},{6,7},{7,4},{8,9},{9,10},{10,1... | collective-permute-start | bytes 3145736 | tf_op jit(solution)/shard_map/ppermute | solution.py:101
  138.0 21.4 %copy-start.2 = (f32[32,64,128]{2,1,0:T(8,128)S(1)}, f32[32,64,128]{2,1,0:T(8,128)}, u32[]{:S(2)}) copy-start(f32[32,64,128]{2,1,0:T(8,128)} %copy-done.1) | copy-start | bytes 3145732
  155.2 5.5 %copy-start.6 = (bf16[4,1,2048]{2,0,1:T(4,128)(2,1)S(1)}, bf16[4,1,2048]{2,0,1:T(4,128)(2,1)}, u32[]{:S(2)}) copy-start(bf16[4,1,2048]{2,0,1:T(4,128)(2,1)} %param.19) | copy-start | bytes 49156
  155.3 5.7 %copy-start.7 = (s32[4,1]{0,1:T(1,128)S(1)}, s32[4,1]{0,1:T(1,128)}, u32[]{:S(2)}) copy-start(s32[4,1]{0,1:T(1,128)} %param.25) | copy-start | bytes 52
  155.3 7.0 %copy-start.8 = (s32[4,1]{0,1:T(1,128)S(1)}, s32[4,1]{0,1:T(1,128)}, u32[]{:S(2)}) copy-start(s32[4,1]{0,1:T(1,128)} %param.24) | copy-start | bytes 52
  155.3 8.3 %copy-start.11 = (f32[4,1,32]{2,1,0:T(1,128)S(1)}, f32[4,1,32]{2,1,0:T(1,128)}, u32[]{:S(2)}) copy-start(f32[4,1,32]{2,1,0:T(1,128)} %param.22) | copy-start | bytes 1540
  155.3 8.3 %copy-start.10 = (bf16[4,1,128]{2,0,1:T(4,128)(2,1)S(1)}, bf16[4,1,128]{2,0,1:T(4,128)(2,1)}, u32[]{:S(2)}) copy-start(bf16[4,1,128]{2,0,1:T(4,128)(2,1)} %param.20) | copy-start | bytes 3076
  160.7 72.0 %all-gather.9.cloned.1.call-start = ((), (), s32[]{:S(2)}) async-start(), calls=%async_computation | async-start | bytes 5242880 | tf_op jit(solution)/shard_map/all_gather | solution.py:114
  198.1 74.5 %all-gather.11.cloned.1.call-start = ((), (), s32[]{:S(2)}) async-start(), calls=%async_computation.1 | async-start | bytes 5242880 | tf_op jit(solution)/shard_map/all_gather | solution.py:114
  199.5 79.7 %copy-start.13 = (u32[32]{0:T(128)S(1)}, u32[32]{0:T(128)}, u32[]{:S(2)}) copy-start(u32[32]{0:T(128)} %constant.142) | copy-start | bytes 388
  199.5 91.5 %copy-start.9 = (f32[4,1]{0,1:T(1,128)S(1)}, f32[4,1]{0,1:T(1,128)}, u32[]{:S(2)}) copy-start(f32[4,1]{0,1:T(1,128)} %param.23) | copy-start | bytes 52
  199.5 153.7 %copy-start.5 = (bf16[256,128]{1,0:T(8,128)(2,1)S(1)}, bf16[256,128]{1,0:T(8,128)(2,1)}, u32[]{:S(2)}) copy-start(bf16[256,128]{1,0:T(8,128)(2,1)} %param.16) | copy-start | bytes 196612
  235.6 1.0 copy-start.3
  237.9 126.5 %all-gather.13.cloned.1.call-start = ((), (), s32[]{:S(2)}) async-start(), calls=%async_computation.2 | async-start | bytes 5242880 | tf_op jit(solution)/shard_map/all_gather | solution.py:114
  275.4 1.0 copy-start.4
  353.9 6.0 %copy-start.12 = (bf16[4,1,128]{2,0,1:T(4,128)(2,1)S(1)}, bf16[4,1,128]{2,0,1:T(4,128)(2,1)}, u32[]{:S(2)}) copy-start(bf16[4,1,128]{2,0,1:T(4,128)(2,1)} %param.21) | copy-start | bytes 3076
Sparse Core Ops, SparseCore 0:
  13.2 83.4 all-gather.14
  160.9 32.9 all-gather.16
  198.2 34.4 all-gather.8
  238.1 34.4 all-gather.10
  278.0 34.5 all-gather.12
